TPU v7x, 512 devices: a whole 4x8x8 slice. The times are simulated.
512 devices in a mesh: vocab: 64 (over z, y), pipe: 8 (over x, core).
Axes of the slice: x: 4, y: 8, z: 8, core: 2. Of those that a mesh axis runs over, the one named last changes fastest.
Arguments:
- hidden_a: bfloat16 [2048, 4096], P('pipe', 'vocab'), parts along dimension 0, may hold values from -8 to 8, as said below
- labels_a: int32 [2048], P('pipe'), parts along dimension 0, may hold values from 0 to 32767
- hidden_b: bfloat16 [2048, 4096], P('pipe', 'vocab'), parts along dimension 0, may hold values from -8 to 8, as said below
- labels_b: int32 [2048], P('pipe'), parts along dimension 0, may hold values from 0 to 32767
- loss_cotangent: float32 [2048], P('pipe'), parts along dimension 0, may hold values from -192 to 192
- out_weight: bfloat16 [32768, 32768], P('pipe', 'vocab'), parts along dimension 0, may hold values from -0.28125 to 0.28125, as said below
Outputs:
- logits_a: bfloat16 [2048, 32768], P('pipe', 'vocab'), parts along dimension 0
- loss_a: float32 [2048], P('pipe'), parts along dimension 0
- amax_scale: float32 [8], P('pipe'), parts along dimension 0
- grad_hidden_b: bfloat16 [2048, 4096], P('pipe', 'vocab'), parts along dimension 0
There are 8 independent parts, one for each index of `pipe`. A program takes and returns all parts, laid end to end along the dimension named above; each array names one. Nothing has to cross between parts.
Inputs may be any that keep to these rules, and one draw needn't show every extreme that they name: `hidden_a`: hidden states of order one. `hidden_b`: hidden states of order one. `out_weight`: entries of scale 3 over the square root of 4096.
All inputs are finite; a program needn't handle non-finite values. Where the computation divides by a largest or mean magnitude, that divisor is 1e-20 or more.
Results may differ from a plain program's by a relative error of at most 0.0048.
Values may be sent and summed in bfloat16 or wider, within the bound.
No kernel may reach another device: no remote copies, remote signals or barrier semaphores. Data moves between devices by JAX's collectives and lax.ppermute only.
A program may use at most 64 MiB of HBM per device.

v0:
```python
import jax
import jax.numpy as jnp
from jax import lax
from jax.sharding import Mesh
from jax.sharding import PartitionSpec as P

VOCAB = ("vocab_0", "vocab_1")


def turned_gather(arrays, axis, dims):
    turned = [jnp.moveaxis(a, dim, 0) for a, dim in zip(arrays, dims)]
    both = jnp.concatenate([t.reshape(len(t), -1) for t in turned], axis=1)
    filled, at, gathered = (lax.all_gather(both, axis, axis=0, tiled=True), 0, [])
    for t, dim in zip(turned, dims):
        slab = filled[:, at : at + t[0].size].reshape(-1, *t.shape[1:])
        gathered.append(jnp.moveaxis(slab, 0, dim))
        at += t[0].size
    return tuple(gathered)


def collected_together(x, axis):
    leaves = jax.tree.leaves(x)
    order = sorted(range(len(leaves)), key=lambda k: -leaves[k].size)
    width = (1, *leaves[order[0]].shape)[-1]
    lines = [
        jnp.pad(leaves[k].reshape(-1), (0, -leaves[k].size % width)).reshape(-1, width)
        for k in order
    ]
    both, at, found = (lax.all_gather(jnp.concatenate(lines), axis), 0, {})
    for k, line in zip(order, lines):
        slab = both[:, at : at + len(line)].reshape(len(both), -1)
        found[k] = slab[:, : leaves[k].size].reshape(-1, *leaves[k].shape)
        at += len(line)
    numbers = iter(range(len(leaves)))
    return jax.tree.map(lambda _: found[next(numbers)], x)


def joined_all(x, axes, combine):
    for axis in axes:
        pieces = collected_together(x, axis)
        x = jax.tree.map(lambda part: part[0], pieces)
        for k in range(1, lax.axis_size(axis)):
            x = combine(x, jax.tree.map(lambda part: part[k], pieces))
    return x


def from_everyone(x, axis):
    devices = lax.axis_size(axis)
    return lax.all_to_all(jnp.broadcast_to(x[None], (devices, *x.shape)), axis, 0, 0, tiled=True)


def all_in_one(x, axis):
    leaves = jax.tree.leaves(x)
    order = sorted(range(len(leaves)), key=lambda k: -leaves[k].size)
    width = (1, *leaves[order[0]].shape)[-1]
    lines = [
        jnp.pad(leaves[k].reshape(-1), (0, -leaves[k].size % width)).reshape(-1, width)
        for k in order
    ]
    both, at, found = (from_everyone(jnp.concatenate(lines), axis), 0, {})
    for k, line in zip(order, lines):
        slab = both[:, at : at + len(line)].reshape(len(both), -1)
        found[k] = slab[:, : leaves[k].size].reshape(-1, *leaves[k].shape)
        at += len(line)
    numbers = iter(range(len(leaves)))
    return jax.tree.map(lambda _: found[next(numbers)], x)


def joined_by_halves(pieces, combine):
    while len(jax.tree.leaves(pieces)[0]) > 1:
        pieces = jax.vmap(combine)(
            *(jax.tree.map(lambda part: part[side::2], pieces) for side in (0, 1))
        )
    return jax.tree.map(lambda part: part[0], pieces)


def merged(x, axis, combine):
    pieces = all_in_one(x, axis)
    return joined_by_halves(pieces, combine)


def scatter_axes(x, axes, dim):
    for axis in axes:
        x = lax.psum_scatter(x, axis, scatter_dimension=dim, tiled=True)
    return x


def combine_forward(earlier, later):
    highest = jnp.maximum(earlier[0], later[0])
    summed = earlier[1] * jnp.exp(earlier[0] - highest) + later[1] * jnp.exp(later[0] - highest)
    return (highest, summed, earlier[2] + later[2], jnp.maximum(earlier[3], later[3]))


def combine_backward(earlier, later):
    highest = jnp.maximum(earlier[0], later[0])
    summed = earlier[1] * jnp.exp(earlier[0] - highest) + later[1] * jnp.exp(later[0] - highest)
    return (highest, summed)


def shards(hidden_a, labels_a, hidden_b, labels_b, loss_cotangent, out_weight):
    vocab_rows = out_weight.shape[1]
    offset = lax.axis_index(VOCAB) * vocab_rows
    portions = turned_gather((hidden_a, hidden_b), VOCAB, (1, 1))
    scores_a = jnp.dot(portions[0], out_weight, preferred_element_type=jnp.float32)
    scores_b = jnp.dot(portions[1], out_weight, preferred_element_type=jnp.float32)
    columns_a = offset + lax.broadcasted_iota(jnp.int32, scores_a.shape, 1)
    columns_b = offset + lax.broadcasted_iota(jnp.int32, scores_b.shape, 1)
    label_local = jnp.sum(jnp.where(columns_a == labels_a[:, None], scores_a, 0.0), axis=1)
    row_peak_a = jnp.max(scores_a, axis=1)
    abs_peak = jnp.max(jnp.abs(scores_a)).reshape(1)
    row_peak_b = jnp.max(scores_b, axis=1)
    own_total_a = jnp.sum(jnp.exp(scores_a - row_peak_a[:, None]), axis=1)
    peak_a, total_a, label_a, largest = joined_all(
        (row_peak_a, own_total_a, label_local, abs_peak), VOCAB, combine_forward
    )
    own_total_b = jnp.sum(jnp.exp(scores_b - row_peak_b[:, None]), axis=1)
    peak_b, total_b = merged((row_peak_b, own_total_b), VOCAB, combine_backward)
    loss_a = jnp.log(total_a) + peak_a - label_a
    amax_scale = (448.0 / largest).astype(jnp.float32)
    onehot = (columns_b == labels_b[:, None]).astype(jnp.float32)
    probs = jnp.exp(scores_b - peak_b[:, None]) / total_b[:, None]
    dlogits_b = ((probs - onehot) * loss_cotangent[:, None]).astype(jnp.bfloat16)
    grad_terms = lax.dot_general(
        dlogits_b, out_weight, (((1,), (1,)), ((), ())), preferred_element_type=jnp.float32
    )
    grad_hidden_b = scatter_axes(grad_terms, VOCAB, 1).astype(jnp.bfloat16)
    return (scores_a.astype(jnp.bfloat16), loss_a, amax_scale, grad_hidden_b)


def solution(mesh):
    finer = Mesh(mesh.devices.reshape(8, 8, mesh.shape["pipe"]), ("vocab_0", "vocab_1", "pipe"))
    placed = (P("pipe", VOCAB), P("pipe"), P("pipe", VOCAB), P("pipe"), P("pipe"), P("pipe", VOCAB))
    return jax.shard_map(
        shards,
        mesh=finer,
        in_specs=placed,
        out_specs=(P("pipe", VOCAB), P("pipe"), P("pipe"), P("pipe", VOCAB)),
        check_vma=False,
    )
```

profile of v0, /device:TPU:2, one launch (start us, length us, event | category | flops | bytes accessed | tf_op | source)
XLA Modules:
  0.0 236.3 jit_solution(9642558782417592460)
XLA Ops:
  7.2 1.4 pad_maximum_fusion
  8.7 94.4 %all-gather.6.cloned.1.call-done = bf16[4096,512]{1,0:T(8,128)(2,1)} async-done(((bf16[64,512]{1,0:T(8,128)(2,1)}), bf16[4096,512]{1,0:T(8,128)(2,1)}) %all-gather.6.cloned.1.call-update) | async-done | bytes 4194320 | tf_op jit(solution)/shard_map/all_gather | solution.py:13
  103.1 4.2 %fusion.61 = (f32[256]{0:T(256)S(1)}, f32[256,512]{1,0:T(8,128)S(1)}) fusion(bf16[4096,512]{1,0:T(8,128)(2,1)} %param.11, bf16[4096,512]{1,0:T(8,128)(2,1)} %all-gather.6.cloned.1.call-done), kind=kOutput, calls=%fused_computation.120 | convolution fusion | flops 1073872640 | bytes 6816768 | tf_op jit(solution)/shard_map/dot_general | solution.py:105
  107.2 0.2 exponential_reduce_fusion
  107.5 0.7 broadcast_in_dim.7
  108.2 8.3 %all-to-all-start = ((f32[64,2,256]{2,1,0:T(2,128)}), f32[64,2,256]{2,1,0:T(2,128)S(1)}, u32[]{:S(2)}, u32[]{:S(2)}) async-start(f32[64,2,256]{2,1,0:T(2,128)} %broadcast_in_dim.7), calls=%async_computation | async-start | bytes 262144 | tf_op jit(solution)/shard_map/all_to_all | solution.py:49
  116.5 0.0 reduce-scatter.5.cloned.1.call-start
  116.6 12.6 %all-to-all-done = f32[64,2,256]{2,1,0:T(2,128)S(1)} async-done(((f32[64,2,256]{2,1,0:T(2,128)}), f32[64,2,256]{2,1,0:T(2,128)S(1)}, u32[]{:S(2)}, u32[]{:S(2)}) %all-to-all-start) | async-done | bytes 131104 | tf_op jit(solution)/shard_map/all_to_all | solution.py:49
  129.2 0.1 fusion.55
  129.9 5.5 %fusion.4 = f32[256,4096]{1,0:T(8,128)} fusion(bf16[4096,512]{1,0:T(8,128)(2,1)} %param.11, f32[256,512]{1,0:T(8,128)S(1)} %get-tuple-element.68, f32[256]{0:T(256)S(1)} %copy-done, f32[256]{0:T(256)S(1)} %bitcast.212, f32[256]{0:T(256)S(1)} %bitcast.213, s32[512]{0:T(512)S(1)} %iota_add_fusion, s32[256]{0:T(256)S(1)} %copy-done.1), kind=kOutput, calls=%fused_computation.9 | convolution fusion | flops 1074659328 | bytes 8919040 | tf_op jit(solution)/shard_map/dot_general | solution.py:123
  135.4 0.0 reduce-scatter.7.cloned.1.call-start
  135.5 4.2 %fusion.60 = (f32[256]{0:T(256)S(1)}, f32[256,512]{1,0:T(8,128)S(1)}) fusion(bf16[4096,512]{1,0:T(8,128)(2,1)} %param.11, bf16[4096,512]{1,0:T(8,128)(2,1)} %all-gather.6.cloned.1.call-done), kind=kOutput, calls=%fused_computation.119 | convolution fusion | flops 1073872640 | bytes 6816768 | tf_op jit(solution)/shard_map/dot_general | solution.py:104
  139.7 1.5 exponential_reduce_fusion.1
  141.2 0.7 pad.7
  141.9 25.2 %all-gather.2 = f32[8,4,256]{2,1,0:T(4,128)S(1)} all-gather(f32[1,4,256]{2,1,0:T(4,128)S(1)} %maximum_bitcast_fusion), channel_id=2, replica_groups=mesh['vocab_0'=8,'vocab_1'=8,'pipe'=8] {'vocab_0'}, dimensions={0}, use_global_device_ids=true | all-gather | bytes 36864 | tf_op jit(solution)/shard_map/all_gather | solution.py:29
  167.1 0.6 fusion.59
  172.8 13.3 %reduce-scatter.5.cloned.1.call-done = f32[256,512]{1,0:T(8,128)} async-done(((f32[256,4096]{1,0:T(8,128)}), f32[256,512]{1,0:T(8,128)}) %reduce-scatter.5.cloned.1.call-update) | async-done | bytes 524304 | tf_op jit(solution)/shard_map/reduce_scatter | solution.py:84
  186.1 2.0 copy.14
  188.2 25.7 %all-gather.3 = f32[8,4,256]{2,1,0:T(4,128)S(1)} all-gather(f32[1,4,256]{2,1,0:T(4,128)S(1)} %maximum_bitcast_fusion.1), channel_id=3, replica_groups=mesh['vocab_0'=8,'vocab_1'=8,'pipe'=8] {'vocab_1'}, dimensions={0}, use_global_device_ids=true | all-gather | bytes 36864 | tf_op jit(solution)/shard_map/all_gather | solution.py:29
  213.9 0.6 fusion.58
  219.6 0.6 add_subtract_fusion
  220.2 6.8 %reduce-scatter.7.cloned.1.call-done = f32[64,256]{1,0:T(8,128)} async-done(((f32[512,256]{1,0:T(8,128)}), f32[64,256]{1,0:T(8,128)}) %reduce-scatter.7.cloned.1.call-update) | async-done | bytes 65552
  227.0 0.9 copy.15
  228.0 0.7 copy.13
  (50 shorter events, 0.7 us)
Async XLA Ops:
  7.2 95.9 %all-gather.6.cloned.1.call-start = ((), (), s32[]{:S(2)}) async-start(), calls=%async_computation.3 | async-start | bytes 4259840 | tf_op jit(solution)/shard_map/all_gather | solution.py:13
  8.6 121.2 %copy-start = (f32[256]{0:T(256)S(1)}, f32[256]{0:T(256)}, u32[]{:S(2)}) copy-start(f32[256]{0:T(256)} %param.10) | copy-start | bytes 3076
  8.7 121.2 %copy-start.1 = (s32[256]{0:T(256)S(1)}, s32[256]{0:T(256)}, u32[]{:S(2)}) copy-start(s32[256]{0:T(256)} %param.9) | copy-start | bytes 3076
  108.2 21.0 %all-to-all-start = ((f32[64,2,256]{2,1,0:T(2,128)}), f32[64,2,256]{2,1,0:T(2,128)S(1)}, u32[]{:S(2)}, u32[]{:S(2)}) async-start(f32[64,2,256]{2,1,0:T(2,128)} %broadcast_in_dim.7), calls=%async_computation | async-start | bytes 262144 | tf_op jit(solution)/shard_map/all_to_all | solution.py:49
  116.5 69.6 %reduce-scatter.5.cloned.1.call-start = ((), (), s32[]{:S(2)}) async-start(), calls=%async_computation.4 | async-start | bytes 4718592 | tf_op jit(solution)/shard_map/reduce_scatter | solution.py:84
  135.4 4.2 %copy-start.2 = (s32[256]{0:T(256)S(1)}, s32[256]{0:T(256)}, u32[]{:S(2)}) copy-start(s32[256]{0:T(256)} %param.7) | copy-start | bytes 3076
  135.4 91.6 %reduce-scatter.7.cloned.1.call-start = ((), (), s32[]{:S(2)}) async-start(), calls=%async_computation.5 | async-start | bytes 589824
Sparse Core Ops, SparseCore 0:
  11.6 91.4 all-gather.5
  135.5 50.5 reduce-scatter.4
  188.9 38.0 reduce-scatter.6
where the time goes:
time: 237 us; the launch traced here: 236 us
  waiting for transfers between devices  127 us (54%)
  blocking collectives  50.9 us (21%)
  between operations  25.2 us (11%)
  matrix products  13.8 us (6%)
  starting transfers between devices  8.44 us (4%)
  local copies, waits for them, and re-layouts  6.81 us (3%)
  other arithmetic  3.99 us (2%)
    all_gather x1, waiting for transfers between devices, turned_gather(): lax.all_gather(both, axis, axis=0, tiled=True)  94.4 us
    all_gather x2, blocking collectives, collected_together(): both, at, found = (lax.all_gather(jnp.concatenate(lines), axis), 0, {})  50.9 us
    reduce_scatter x1, waiting for transfers between devices, scatter_axes(): x = lax.psum_scatter(x, axis, scatter_dimension=dim, tiled=True)  13.3 us
    all_to_all x1, waiting for transfers between devices, from_everyone(): lax.all_to_all(jnp.broadcast_to(x[None], (devices, *x.shape)), axis, 0, 0...  12.6 us
    all_to_all x1, starting transfers between devices, from_everyone(): lax.all_to_all(jnp.broadcast_to(x[None], (devices, *x.shape)), axis, 0, 0...  8.32 us
    unnamed x4, waiting for transfers between devices  6.9 us
    dot_general x1, matrix products, shards(): lax.dot_general(dlogits_b, out_weight, (((1,), (1,)), ((), ())), preferre...  5.51 us
  transfers between devices with their start and end apart: 4, of which 4 were waited for; matrix products, arithmetic and copies ran while one was open for 4% of the time, Pallas kernels for 0%

commit v1 on v0

--- a/solution.py
+++ b/solution.py
@@ -10,7 +10,17 @@
 def turned_gather(arrays, axis, dims):
     turned = [jnp.moveaxis(a, dim, 0) for a, dim in zip(arrays, dims)]
     both = jnp.concatenate([t.reshape(len(t), -1) for t in turned], axis=1)
-    filled, at, gathered = (lax.all_gather(both, axis, axis=0, tiled=True), 0, [])
+
+    def _assign_panels(local_values, dim_no):
+        mixed_arr = jnp.concatenate(
+            lax.all_to_all(
+                jnp.stack(tuple((local_values for _ in range(lax.axis_size(axis))))), axis, 0, 0
+            ),
+            axis=dim_no,
+        )
+        return mixed_arr
+
+    filled, at, gathered = (_assign_panels(both, 0), 0, [])
     for t, dim in zip(turned, dims):
         slab = filled[:, at : at + t[0].size].reshape(-1, *t.shape[1:])
         gathered.append(jnp.moveaxis(slab, 0, dim))

time: 237 us -> 259 us (1.093)
  the two profiles are of different devices: /device:TPU:2 before, /device:TPU:4 now
where the time goes in v1:
time: 259 us
  blocking collectives  165 us (64%)
  waiting for transfers between devices  32.9 us (13%)
  between operations  25.5 us (10%)
  starting transfers between devices  12.7 us (5%)
  matrix products  11 us (4%)
  local copies, waits for them, and re-layouts  7.87 us (3%)
  other arithmetic  3.36 us (1%)
    all_to_all x1, blocking collectives, _assign_panels(): lax.all_to_all(jnp.stack(tuple((local_values for _ in range(lax.axis_size...  114 us
    all_gather x2, blocking collectives, collected_together(): both, at, found = (lax.all_gather(jnp.concatenate(lines), axis), 0, {})  50.9 us
    reduce_scatter x1, waiting for transfers between devices, scatter_axes(): x = lax.psum_scatter(x, axis, scatter_dimension=dim, tiled=True)  13.4 us
    all_to_all x1, waiting for transfers between devices, from_everyone(): lax.all_to_all(jnp.broadcast_to(x[None], (devices, *x.shape)), axis, 0, 0...  12.7 us
    all_to_all x1, starting transfers between devices, from_everyone(): lax.all_to_all(jnp.broadcast_to(x[None], (devices, *x.shape)), axis, 0, 0...  12.6 us
    unnamed x3, waiting for transfers between devices  6.83 us
    dot_general x1, matrix products, shards(): lax.dot_general(dlogits_b, out_weight, (((1,), (1,)), ((), ())), preferre...  5.49 us
  transfers between devices with their start and end apart: 3, of which 3 were waited for; matrix products, arithmetic and copies ran while one was open for 3% of the time, Pallas kernels for 0%

profile of v1, /device:TPU:4, one launch (start us, length us, event | category | flops | bytes accessed | tf_op | source)
XLA Modules:
  0.0 258.5 jit_solution(7130072115704097422)
XLA Ops:
  7.2 0.8 pad_maximum_fusion
  7.9 0.5 stack.2
  8.5 114.4 %all_to_all.10 = bf16[64,64,512]{2,1,0:T(8,128)(2,1)S(1)} all-to-all(bf16[64,64,512]{2,1,0:T(8,128)(2,1)S(1)} %stack.2), channel_id=1, replica_groups=mesh['vocab_0'=8,'vocab_1'=8,'pipe'=8] {'vocab_0','vocab_1'}, dimensions={0} | all-to-all | bytes 8388608 | tf_op jit(solution)/shard_map/all_to_all | solution.py:16
  122.8 1.3 fusion.61
  124.2 0.6 copy-done.1
  124.8 0.2 exponential_reduce_fusion
  125.0 0.7 broadcast_in_dim.7
  125.7 12.6 %all-to-all-start.1 = ((f32[64,2,256]{2,1,0:T(2,128)}), f32[64,2,256]{2,1,0:T(2,128)S(1)}, u32[]{:S(2)}, u32[]{:S(2)}) async-start(f32[64,2,256]{2,1,0:T(2,128)} %broadcast_in_dim.7), calls=%async_computation.1 | async-start | bytes 262144 | tf_op jit(solution)/shard_map/all_to_all | solution.py:59
  138.4 12.7 %all-to-all-done.1 = f32[64,2,256]{2,1,0:T(2,128)S(1)} async-done(((f32[64,2,256]{2,1,0:T(2,128)}), f32[64,2,256]{2,1,0:T(2,128)S(1)}, u32[]{:S(2)}, u32[]{:S(2)}) %all-to-all-start.1) | async-done | bytes 131104 | tf_op jit(solution)/shard_map/all_to_all | solution.py:59
  151.1 0.1 fusion.55
  151.7 5.5 %fusion.4 = f32[256,4096]{1,0:T(8,128)} fusion(bf16[4096,512]{1,0:T(8,128)(2,1)} %param.11, f32[256,512]{1,0:T(8,128)S(1)} %get-tuple-element.68, f32[256]{0:T(256)S(1)} %copy-done.2, f32[256]{0:T(256)S(1)} %bitcast.215, f32[256]{0:T(256)S(1)} %bitcast.216, s32[512]{0:T(512)S(1)} %iota_add_fusion, s32[256]{0:T(256)S(1)} %copy-done.3), kind=kOutput, calls=%fused_computation.9 | convolution fusion | flops 1074659328 | bytes 8919040 | tf_op jit(solution)/shard_map/dot_general | solution.py:133
  157.3 4.2 %fusion.60 = (f32[256]{0:T(256)S(1)}, f32[256,512]{1,0:T(8,128)S(1)}) fusion(bf16[4096,512]{1,0:T(8,128)(2,1)} %param.11, bf16[4096,512]{1,0:T(8,128)(2,1)} %bitcast.210), kind=kOutput, calls=%fused_computation.119 | convolution fusion | flops 1073872640 | bytes 6816768 | tf_op jit(solution)/shard_map/dot_general | solution.py:114
  161.5 1.5 exponential_reduce_fusion.1
  163.0 0.6 pad.7
  163.7 25.2 %all-gather.2 = f32[8,4,256]{2,1,0:T(4,128)S(1)} all-gather(f32[1,4,256]{2,1,0:T(4,128)S(1)} %maximum_bitcast_fusion), channel_id=2, replica_groups=mesh['vocab_0'=8,'vocab_1'=8,'pipe'=8] {'vocab_0'}, dimensions={0}, use_global_device_ids=true | all-gather | bytes 36864 | tf_op jit(solution)/shard_map/all_gather | solution.py:39
  189.0 0.6 fusion.59
  194.6 13.4 %reduce-scatter.5.cloned.1.call-done = f32[256,512]{1,0:T(8,128)} async-done(((f32[256,4096]{1,0:T(8,128)}), f32[256,512]{1,0:T(8,128)}) %reduce-scatter.5.cloned.1.call-update) | async-done | bytes 524304 | tf_op jit(solution)/shard_map/reduce_scatter | solution.py:94
  207.9 2.0 copy.14
  210.0 25.7 %all-gather.3 = f32[8,4,256]{2,1,0:T(4,128)S(1)} all-gather(f32[1,4,256]{2,1,0:T(4,128)S(1)} %maximum_bitcast_fusion.1), channel_id=3, replica_groups=mesh['vocab_0'=8,'vocab_1'=8,'pipe'=8] {'vocab_1'}, dimensions={0}, use_global_device_ids=true | all-gather | bytes 36864 | tf_op jit(solution)/shard_map/all_gather | solution.py:39
  235.7 0.6 fusion.58
  241.5 0.6 add_subtract_fusion
  242.1 6.8 %reduce-scatter.7.cloned.1.call-done = f32[64,256]{1,0:T(8,128)} async-done(((f32[512,256]{1,0:T(8,128)}), f32[64,256]{1,0:T(8,128)}) %reduce-scatter.7.cloned.1.call-update) | async-done | bytes 65552
  248.9 0.9 copy.15
  249.8 0.7 copy.13
  (53 shorter events, 0.8 us)
Async XLA Ops:
  8.4 114.4 %copy-start = (bf16[4096,512]{1,0:T(8,128)(2,1)S(1)}, bf16[4096,512]{1,0:T(8,128)(2,1)}, u32[]{:S(2)}) copy-start(bf16[4096,512]{1,0:T(8,128)(2,1)} %param.11) | copy-start | bytes 12582916
  122.8 2.0 copy-start.1
  122.8 28.9 %copy-start.2 = (f32[256]{0:T(256)S(1)}, f32[256]{0:T(256)}, u32[]{:S(2)}) copy-start(f32[256]{0:T(256)} %param.10) | copy-start | bytes 3076
  122.8 28.9 %copy-start.3 = (s32[256]{0:T(256)S(1)}, s32[256]{0:T(256)}, u32[]{:S(2)}) copy-start(s32[256]{0:T(256)} %param.9) | copy-start | bytes 3076
  125.7 25.3 %all-to-all-start.1 = ((f32[64,2,256]{2,1,0:T(2,128)}), f32[64,2,256]{2,1,0:T(2,128)S(1)}, u32[]{:S(2)}, u32[]{:S(2)}) async-start(f32[64,2,256]{2,1,0:T(2,128)} %broadcast_in_dim.7), calls=%async_computation.1 | async-start | bytes 262144 | tf_op jit(solution)/shard_map/all_to_all | solution.py:59
  138.3 69.6 %reduce-scatter.5.cloned.1.call-start = ((), (), s32[]{:S(2)}) async-start(), calls=%async_computation.4 | async-start | bytes 4718592 | tf_op jit(solution)/shard_map/reduce_scatter | solution.py:94
  157.3 4.2 %copy-start.4 = (s32[256]{0:T(256)S(1)}, s32[256]{0:T(256)}, u32[]{:S(2)}) copy-start(s32[256]{0:T(256)} %param.7) | copy-start | bytes 3076
  157.3 91.6 %reduce-scatter.7.cloned.1.call-start = ((), (), s32[]{:S(2)}) async-start(), calls=%async_computation.5 | async-start | bytes 589824
Sparse Core Ops, SparseCore 0:
  157.4 50.5 reduce-scatter.4
  210.7 38.0 reduce-scatter.6
